TPU v7x, 32 devices: a whole 2x2x4 slice. The times are simulated.
32 devices in a mesh: groups: 2 (over y), dom: 4 (over z), ens: 4 (over x, core).
Axes of the slice: x: 2, y: 2, z: 4, core: 2. Of those that a mesh axis runs over, the one named last changes fastest.
Arguments:
- state: float32 [16, 256, 512], P('ens', ('groups', 'dom')), parts along dimension 1, may hold values from -8 to 8, as said below
- coords: float32 [3, 2048], P(None, ('groups', 'dom')), parts along dimension 1, may hold values from -1 to 1
- owner_local: int32 [2048], P(('groups', 'dom')), parts along dimension 0, may hold values from 0 to 31
- counts: int32 [8, 4], P(('groups', 'dom')), parts along dimension 0, may hold values from 32 to 64, as said below
- obs_value: float32 [2048], P(('groups', 'dom')), parts along dimension 0, may hold values from 0.5 to 3.5
- obs_weight: float32 [2048], P(('groups', 'dom')), parts along dimension 0, as said below
Outputs:
- analysis: float32 [16, 256, 512], P('ens', ('groups', 'dom')), parts along dimension 1
There are 2 independent parts, one for each index of `groups`. A program takes and returns all parts, laid end to end along the dimension named above; each array names one. Nothing has to cross between parts.
Inputs may be any that keep to these rules, and one draw needn't show every extreme that they name: `state`: each member is an independent field plus an offset of its own. The sensors of one block are stored in order of owner block: the first counts[d, 0] slots belong to owner block 0, the next counts[d, 1] to block 1, and so on; slots after the last of them are unused. For one owner block, chosen by the draw, every row holds exactly 64. `obs_weight`: Positive.
All inputs are finite; a program needn't handle non-finite values.
Results may differ from a plain program's by a relative error of at most 0.00028.
Values sent between devices are 32-bit elements; how exact they have to be, the bound alone decides.
A program may use at most 64 MiB of HBM per device.

v0:
```python
import functools

import jax
import jax.numpy as jnp
from jax import lax
from jax.experimental import pallas as pl
from jax.experimental.pallas import tpu as pltpu
from jax.sharding import PartitionSpec as P

NS_ITERS = 8
GLL_POINTS = (
    -1.0,
    -0.8717401485096066,
    -0.5917001814331423,
    -0.2092992179024789,
    0.2092992179024789,
    0.5917001814331423,
    0.8717401485096066,
    1.0,
)
INFLATION = 1.1
LANES = 128
FOUR = 4
MESH = pl.DeviceIdType.MESH
F32 = jnp.float32
BF16 = jnp.bfloat16


def each(count, body):
    if count <= 8:
        for index in range(count):
            body(index)
    else:
        lax.fori_loop(0, count, lambda index, _: (body(index), 0)[1], 0)


def halves(value):
    high = value.astype(BF16)
    return high, (value - high.astype(F32)).astype(BF16)


def dot(a, b, contract=((1,), (0,))):
    return lax.dot_general(
        a,
        b,
        (contract, ((), ())),
        precision=lax.Precision.HIGHEST,
        preferred_element_type=F32,
    )


def lagrange(position):
    shape = (8, position.shape[1])
    row = lax.broadcasted_iota(jnp.int32, shape, 0)
    x = jnp.broadcast_to(position, shape)
    product = jnp.zeros(shape, F32)
    for a in range(8):
        scale = 1.0
        for b in range(8):
            if b != a:
                scale /= GLL_POINTS[a] - GLL_POINTS[b]
        product = jnp.where(row == a, scale, product)
    for b in range(8):
        product = product * jnp.where(row == b, 1.0, x - GLL_POINTS[b])
    return product


def kernel(
    n_dom,
    n_ens,
    counts_hbm,
    coords_hbm,
    owner_hbm,
    value_hbm,
    weight_hbm,
    state_ref,
    out_ref,
    counts_ref,
    coords_ref,
    owner_ref,
    value_ref,
    weight_ref,
    packed,
    sensors,
    gathered,
    state_high,
    state_low,
    values,
    partial,
    mix_rows,
    small_sem,
    load_sem,
    sensor_send,
    sensor_recv,
    value_send,
    value_recv,
    part_send,
    part_recv,
    near_sem,
    far_send,
    far_recv,
    pass_send,
    pass_recv,
):
    d = lax.axis_index("dom")
    e = lax.axis_index("ens")
    local_members, local_elements, nodes = state_ref.shape
    members = local_members * n_ens
    slots = coords_hbm.shape[1]
    cap = slots // n_dom
    near = e + 1 - 2 * lax.rem(e, 2)
    far = lax.rem(e + 2, n_ens)

    barrier = pltpu.get_barrier_semaphore()
    for axis, me, count in (("dom", d, n_dom), ("ens", e, n_ens)):
        for off in range(1, count):
            pl.semaphore_signal(
                barrier, inc=1, device_id={axis: lax.rem(me + off, count)}, device_id_type=MESH
            )
    small = [
        pltpu.make_async_copy(source, target, small_sem.at[index])
        for index, (source, target) in enumerate(
            (
                (counts_hbm, counts_ref),
                (coords_hbm, coords_ref),
                (owner_hbm, owner_ref),
                (value_hbm, value_ref),
                (weight_hbm, weight_ref),
            )
        )
    ]
    for copy in small:
        copy.start()
    load = pltpu.make_async_copy(state_ref, gathered.at[e], load_sem)
    load.start()
    for copy in small:
        copy.wait()

    zero = jnp.zeros((2, slots), F32)
    feature = jnp.concatenate(
        [
            coords_ref[...],
            owner_ref[...].astype(F32),
            value_ref[...],
            weight_ref[...],
            zero,
        ],
        axis=0,
    )
    slot = lax.broadcasted_iota(jnp.int32, (slots, LANES), 0)
    lane = lax.broadcasted_iota(jnp.int32, (slots, LANES), 1) - lax.rem(d, 2) * cap

    def pack(q, start):
        count = counts_ref[0, q]
        wanted = jnp.where((lane >= 0) & (lane < count), lane + start, -1)
        packed[q] = dot(feature, (slot == wanted).astype(F32))
        return start + count

    if n_dom <= 8:
        start = jnp.int32(0)
        for q in range(n_dom):
            start = pack(q, start)
    else:
        lax.fori_loop(0, n_dom, pack, jnp.int32(0))
    sensors[d] = packed[d]

    load.wait()
    high, low = halves(gathered[e].reshape(local_members * local_elements, nodes))
    state_high[...] = high
    state_low[...] = low

    pl.semaphore_wait(barrier, n_dom - 1 + n_ens - 1)

    def sensor_copy(off):
        to = lax.rem(d + off, n_dom)
        return pltpu.make_async_remote_copy(
            src_ref=packed.at[to],
            dst_ref=sensors.at[d],
            send_sem=sensor_send.at[off],
            recv_sem=sensor_recv.at[off],
            device_id={"dom": to},
            device_id_type=MESH,
        )

    def far_copy(m):
        return pltpu.make_async_remote_copy(
            src_ref=gathered.at[e, m],
            dst_ref=gathered.at[e, m],
            send_sem=far_send.at[m],
            recv_sem=far_recv.at[m],
            device_id={"ens": far},
            device_id_type=MESH,
        )

    def pass_copy(m):
        return pltpu.make_async_remote_copy(
            src_ref=gathered.at[far, m],
            dst_ref=gathered.at[far, m],
            send_sem=pass_send.at[m],
            recv_sem=pass_recv.at[m],
            device_id={"ens": near},
            device_id_type=MESH,
        )

    near_copy = pltpu.make_async_remote_copy(
        src_ref=gathered.at[e],
        dst_ref=gathered.at[e],
        send_sem=near_sem.at[0],
        recv_sem=near_sem.at[1],
        device_id={"ens": near},
        device_id_type=MESH,
    )

    each(n_dom - 1, lambda i: sensor_copy(i + 1).start())
    early = local_members // 2
    for m in range(early):
        far_copy(m).start()
    near_copy.start()
    each(n_dom - 1, lambda i: sensor_copy(i + 1).wait_recv())

    width = FOUR * cap
    value_row = lax.broadcasted_iota(jnp.int32, (8, width), 0) - lax.rem(e * local_members, 8)
    element = lax.broadcasted_iota(jnp.int32, (local_elements, width), 0).astype(F32)

    def columns(c):
        return jnp.concatenate(
            [
                sensors[c * FOUR + 2 * pair] + sensors[c * FOUR + 2 * pair + 1]
                for pair in range(FOUR // 2)
            ],
            axis=1,
        )

    def interpolate(c):
        data = columns(c)
        along_r = lagrange(data[0:1])
        along_s = lagrange(data[1:2])
        along_t = lagrange(data[2:3])
        table = []
        for t in range(8):
            for s in range(8):
                table.append(along_r * (along_s[s : s + 1] * along_t[t : t + 1]))
        table_high, table_low = halves(jnp.concatenate(table, axis=0))
        product = functools.partial(jnp.dot, preferred_element_type=F32)
        found = product(state_high[...], table_high) + (
            product(state_high[...], table_low) + product(state_low[...], table_high)
        )
        mine = element == data[3:4]
        block = jnp.zeros((8, width), F32)
        for m in range(local_members):
            rows = found[m * local_elements : (m + 1) * local_elements]
            chosen = jnp.sum(jnp.where(mine, rows, 0.0), axis=0, keepdims=True)
            block = jnp.where(value_row == m, chosen, block)
        values[e, c] = block

    chunks = n_dom // FOUR
    each(chunks, interpolate)

    def value_copy(off):
        return pltpu.make_async_remote_copy(
            src_ref=values.at[e],
            dst_ref=values.at[e],
            send_sem=value_send.at[off],
            recv_sem=value_recv.at[off],
            device_id={"ens": lax.rem(e + off, n_ens)},
            device_id_type=MESH,
        )

    for off in range(1, n_ens):
        value_copy(off).start()
    for m in range(early, local_members):
        far_copy(m).start()
    for m in range(early):
        far_copy(m).wait_recv()
        pass_copy(m).start()
    for off in range(1, n_ens):
        value_copy(off).wait_recv()

    share = 8 // local_members

    def products(c, sums):
        data = columns(c)
        rows = []
        for first in range(0, n_ens, share):
            tile = values[first, c]
            for other in range(1, share):
                tile = tile + values[first + other, c]
            rows.append(tile)
        model = jnp.concatenate(rows, axis=0)
        mean_value = jnp.mean(model, axis=0, keepdims=True)
        anomaly = model - mean_value
        weighted = anomaly * data[5:6]
        innovation = jnp.broadcast_to(data[4:5] - mean_value, anomaly.shape)
        square = jnp.sum(weighted * anomaly, keepdims=True)
        both = jnp.concatenate([anomaly, innovation], axis=0)
        return sums[0] + dot(weighted, both, ((1,), (1,))), sums[1] + square

    none = (jnp.zeros((members, 2 * members), F32), jnp.zeros((1, 1), F32))
    if chunks == 1:
        sums = products(0, none)
    else:
        sums = lax.fori_loop(0, chunks, products, none)
    partial[d, :, 0 : 2 * members] = sums[0]
    partial[d, :, 2 * members : 3 * members] = jnp.broadcast_to(sums[1], (members, members))

    def part_copy(off):
        return pltpu.make_async_remote_copy(
            src_ref=partial.at[d],
            dst_ref=partial.at[d],
            send_sem=part_send.at[off],
            recv_sem=part_recv.at[off],
            device_id={"dom": lax.rem(d + off, n_dom)},
            device_id_type=MESH,
        )

    each(n_dom - 1, lambda i: part_copy(i + 1).start())
    for m in range(early, local_members):
        far_copy(m).wait_recv()
        pass_copy(m).start()
    each(n_dom - 1, lambda i: part_copy(i + 1).wait_recv())

    if n_dom <= 8:
        total = partial[0]
        for q in range(1, n_dom):
            total = total + partial[q]
    else:
        total = lax.fori_loop(
            0, n_dom, lambda q, sums: sums + partial[q], jnp.zeros((members, LANES), F32)
        )
    cross_terms = total[:, 0:members]
    project = total[:, members : 2 * members]
    row = lax.broadcasted_iota(jnp.int32, (members, members), 0)
    column = lax.broadcasted_iota(jnp.int32, (members, members), 1)
    identity = (row == column).astype(F32)
    system = cross_terms + (members - 1) / INFLATION * identity
    shift = members * ((members - 1) / INFLATION)
    trace_value = total[:, 2 * members : 3 * members] + shift
    scaled = system / trace_value
    middle = 1.5 * identity - 0.5 * scaled
    both = jnp.concatenate([dot(scaled, middle), middle], axis=0)
    for sweep in range(1, NS_ITERS):
        middle = 1.5 * identity - 0.5 * dot(both[members:], both[:members])
        both = dot(both, middle)
    inverse_root = both[members:]
    mean_weights = dot(inverse_root, dot(inverse_root, project)) / trace_value
    transform = inverse_root * jnp.sqrt((members - 1) / trace_value) + mean_weights
    mixing = transform - jnp.mean(transform, axis=0, keepdims=True) + 1.0 / members

    spread = (members, local_members * LANES)
    pick = lax.broadcasted_iota(jnp.int32, spread, 0) == (
        lax.broadcasted_iota(jnp.int32, spread, 1) // LANES + e * local_members
    )
    pick = pick.astype(BF16)
    high, low = halves(mixing)
    product = functools.partial(jnp.dot, preferred_element_type=F32)
    mix_rows[...] = product(high, pick) + product(low, pick)

    near_copy.wait_recv()
    for m in range(local_members):
        pass_copy(m).wait_recv()

    for part in range(nodes // LANES):
        where = slice(part * LANES, (part + 1) * LANES)
        sums = [None] * local_members
        for j in range(members):
            field = gathered[j // local_members, j % local_members, :, where]
            for k in range(local_members):
                term = mix_rows[j : j + 1, k * LANES : (k + 1) * LANES] * field
                sums[k] = term if sums[k] is None else sums[k] + term
        for k in range(local_members):
            out_ref[k, :, where] = sums[k]

    each(n_dom - 1, lambda i: sensor_copy(i + 1).wait_send())
    each(n_dom - 1, lambda i: part_copy(i + 1).wait_send())
    for off in range(1, n_ens):
        value_copy(off).wait_send()
    near_copy.wait_send()
    for m in range(local_members):
        far_copy(m).wait_send()
        pass_copy(m).wait_send()


def on_device(n_dom, n_ens, state, coords, owner_local, counts, obs_value, obs_weight):
    local_members, local_elements, nodes = state.shape
    slots = coords.shape[1]
    width = FOUR * (slots // n_dom)
    members = local_members * n_ens
    rows = local_members * local_elements
    dma = pltpu.SemaphoreType.DMA
    return pl.pallas_call(
        functools.partial(kernel, n_dom, n_ens),
        out_shape=pltpu.VMEM(state.shape, F32),
        in_specs=[pl.BlockSpec(memory_space=pl.ANY)] * 6,
        out_specs=pl.BlockSpec(memory_space=pltpu.VMEM),
        scratch_shapes=[
            pltpu.SMEM((1, n_dom), jnp.int32),
            pltpu.VMEM(coords.shape, F32),
            pltpu.VMEM((1, slots), jnp.int32),
            pltpu.VMEM((1, slots), F32),
            pltpu.VMEM((1, slots), F32),
            pltpu.VMEM((n_dom, 8, LANES), F32),
            pltpu.VMEM((n_dom, 8, LANES), F32),
            pltpu.VMEM((n_ens,) + state.shape, F32),
            pltpu.VMEM((rows, nodes), BF16),
            pltpu.VMEM((rows, nodes), BF16),
            pltpu.VMEM((n_ens, n_dom // FOUR, 8, width), F32),
            pltpu.VMEM((n_dom, members, LANES), F32),
            pltpu.VMEM((members, local_members * LANES), F32),
            dma((5,)),
            dma,
            dma((n_dom,)),
            dma((n_dom,)),
            dma((n_ens,)),
            dma((n_ens,)),
            dma((n_dom,)),
            dma((n_dom,)),
            dma((2,)),
            dma((local_members,)),
            dma((local_members,)),
            dma((local_members,)),
            dma((local_members,)),
        ],
        compiler_params=pltpu.CompilerParams(collective_id=0, has_side_effects=True),
        name="analysis",
    )(
        counts,
        coords,
        owner_local.reshape(1, slots),
        obs_value.reshape(1, slots),
        obs_weight.reshape(1, slots),
        state,
    )


def solution(mesh):
    return jax.shard_map(
        functools.partial(on_device, mesh.shape["dom"], mesh.shape["ens"]),
        mesh=mesh,
        in_specs=(
            P("ens", ("groups", "dom"), None),
            P(None, ("groups", "dom")),
            P(("groups", "dom")),
            P(("groups", "dom"), None),
            P(("groups", "dom")),
            P(("groups", "dom")),
        ),
        out_specs=P("ens", ("groups", "dom"), None),
        check_vma=False,
    )
```

profile of v0, /device:TPU:0, one launch (start us, length us, event | category | flops | bytes accessed | tf_op | source)
XLA Modules:
  0.0 20.1 jit_solution(12384221096237713314)
XLA Ops:
  0.0 19.4 %analysis.1 = f32[4,32,512]{2,1,0:T(8,128)S(1)} custom-call(s32[1,4]{1,0:T(1,128)} %counts_hbm.1, f32[3,256]{1,0:T(4,128)} %coords_hbm.1, s32[1,256]{1,0:T(1,128)} %bitcast.3, f32[1,256]{1,0:T(1,128)} %bitcast.4, f32[1,256]{1,0:T(1,128)} %bitcast.5, f32[4,32,512]{2,1,0:T(8,128)} %state_ref.1), custom_call_target="tpu_custom_call" | custom-call | tf_op jit(solution)/shard_map/analysis/pallas_call | solution.py:390
  19.4 0.7 %copy.8 = f32[4,32,512]{2,1,0:T(8,128)} copy(f32[4,32,512]{2,1,0:T(8,128)S(1)} %analysis.1) | data formatting | bytes 524288
where the time goes:
time: 20.3 us; the launch traced here: 20.1 us
  Pallas kernels  19.4 us (96%)
  local copies, waits for them, and re-layouts  0.71 us (3%)
    pallas_call x1, Pallas kernels, on_device(): pl.pallas_call(functools.partial(kernel, n_dom, n_ens), out_shape=pltpu.V...  19.4 us
    unnamed x1, local copies, waits for them, and re-layouts  0.71 us

commit v1 on v0

--- a/solution.py
+++ b/solution.py
@@ -300,8 +300,8 @@
         sums = products(0, none)
     else:
         sums = lax.fori_loop(0, chunks, products, none)
-    partial[d, :, 0 : 2 * members] = sums[0]
-    partial[d, :, 2 * members : 3 * members] = jnp.broadcast_to(sums[1], (members, members))
+    partial[d, 0:members, 0 : 2 * members] = sums[0]
+    partial[d, members:, :] = jnp.broadcast_to(sums[1], (8, LANES))
 
     def part_copy(off):
         return pltpu.make_async_remote_copy(
@@ -325,35 +325,43 @@
             total = total + partial[q]
     else:
         total = lax.fori_loop(
-            0, n_dom, lambda q, sums: sums + partial[q], jnp.zeros((members, LANES), F32)
-        )
-    cross_terms = total[:, 0:members]
-    project = total[:, members : 2 * members]
-    row = lax.broadcasted_iota(jnp.int32, (members, members), 0)
-    column = lax.broadcasted_iota(jnp.int32, (members, members), 1)
-    identity = (row == column).astype(F32)
-    system = cross_terms + (members - 1) / INFLATION * identity
-    shift = members * ((members - 1) / INFLATION)
-    trace_value = total[:, 2 * members : 3 * members] + shift
-    scaled = system / trace_value
-    middle = 1.5 * identity - 0.5 * scaled
-    both = jnp.concatenate([dot(scaled, middle), middle], axis=0)
-    for sweep in range(1, NS_ITERS):
-        middle = 1.5 * identity - 0.5 * dot(both[members:], both[:members])
-        both = dot(both, middle)
-    inverse_root = both[members:]
-    mean_weights = dot(inverse_root, dot(inverse_root, project)) / trace_value
-    transform = inverse_root * jnp.sqrt((members - 1) / trace_value) + mean_weights
+            0, n_dom, lambda q, sums: sums + partial[q], jnp.zeros((members + 8, LANES), F32)
+        )
+    shape = (members, LANES)
+    row = lax.broadcasted_iota(jnp.int32, shape, 0)
+    lane = lax.broadcasted_iota(jnp.int32, shape, 1)
+    diagonal = (row == lane).astype(F32)
+    ridge = (members - 1) / INFLATION
+    trace_value = jnp.concatenate(
+        [total[members : members + 8]] * (members // 8), axis=0
+    ) + members * ridge
+    total = total[:members]
+    system = jnp.where(lane < members, total + ridge * diagonal, total)
+    squared = jnp.where(lane < members, system / trace_value, total)
+    single = (row + members == lane + e * local_members).astype(F32)
+    for sweep in range(NS_ITERS):
+        middle = 1.5 * diagonal - 0.5 * squared
+        columns_of = [
+            jnp.broadcast_to(middle[:, k : k + 1], shape) for k in range(members)
+        ]
+
+        def times(operand):
+            terms = [
+                columns_of[k] * jnp.broadcast_to(operand[k : k + 1, :], shape)
+                for k in range(members)
+            ]
+            while len(terms) > 1:
+                terms = [terms[i] + terms[i + 1] for i in range(0, len(terms), 2)]
+            return terms[0]
+
+        squared = times(times(squared))
+        single = times(single)
+    transform = single * jnp.sqrt((members - 1) / trace_value) + squared / trace_value
     mixing = transform - jnp.mean(transform, axis=0, keepdims=True) + 1.0 / members
-
-    spread = (members, local_members * LANES)
-    pick = lax.broadcasted_iota(jnp.int32, spread, 0) == (
-        lax.broadcasted_iota(jnp.int32, spread, 1) // LANES + e * local_members
-    )
-    pick = pick.astype(BF16)
-    high, low = halves(mixing)
-    product = functools.partial(jnp.dot, preferred_element_type=F32)
-    mix_rows[...] = product(high, pick) + product(low, pick)
+    for k in range(local_members):
+        mix_rows[:, k * LANES : (k + 1) * LANES] = jnp.broadcast_to(
+            mixing[:, members + k : members + k + 1], shape
+        )
 
     near_copy.wait_recv()
     for m in range(local_members):
@@ -404,7 +412,7 @@
             pltpu.VMEM((rows, nodes), BF16),
             pltpu.VMEM((rows, nodes), BF16),
             pltpu.VMEM((n_ens, n_dom // FOUR, 8, width), F32),
-            pltpu.VMEM((n_dom, members, LANES), F32),
+            pltpu.VMEM((n_dom, members + 8, LANES), F32),
             pltpu.VMEM((members, local_members * LANES), F32),
             dma((5,)),
             dma,

time: 20.3 us -> 18.7 us (0.921)
  Pallas kernels: 19.4 us -> 17.9 us
    pallas_call x1, Pallas kernels: 19.4 us -> 17.9 us  [on_device(): pl.pallas_call(functools.partial(kernel, n_dom, n_ens), out_shape=pltpu.V...]
where the time goes in v1:
time: 18.7 us; the launch traced here: 18.6 us
  Pallas kernels  17.9 us (96%)
  local copies, waits for them, and re-layouts  0.71 us (4%)
    pallas_call x1, Pallas kernels, on_device(): pl.pallas_call(functools.partial(kernel, n_dom, n_ens), out_shape=pltpu.V...  17.9 us
    unnamed x1, local copies, waits for them, and re-layouts  0.71 us

profile of v1, /device:TPU:0, one launch (start us, length us, event | category | flops | bytes accessed | tf_op | source)
XLA Modules:
  0.0 18.6 jit_solution(9969339155181672572)
XLA Ops:
  0.0 17.9 %analysis.1 = f32[4,32,512]{2,1,0:T(8,128)S(1)} custom-call(s32[1,4]{1,0:T(1,128)} %counts_hbm.1, f32[3,256]{1,0:T(4,128)} %coords_hbm.1, s32[1,256]{1,0:T(1,128)} %bitcast.3, f32[1,256]{1,0:T(1,128)} %bitcast.4, f32[1,256]{1,0:T(1,128)} %bitcast.5, f32[4,32,512]{2,1,0:T(8,128)} %state_ref.1), custom_call_target="tpu_custom_call" | custom-call | tf_op jit(solution)/shard_map/analysis/pallas_call | solution.py:398
  17.9 0.7 %copy.8 = f32[4,32,512]{2,1,0:T(8,128)} copy(f32[4,32,512]{2,1,0:T(8,128)S(1)} %analysis.1) | data formatting | bytes 524288
